TPU v7x, 32 devices: a whole 2x2x4 slice. The times are simulated.
32 devices in a mesh: gx: 2 (over x), gy: 4 (over y, core), gz: 4 (over z).
Axes of the slice: x: 2, y: 2, z: 4, core: 2. Of those that a mesh axis runs over, the one named last changes fastest.
Arguments:
- features: bfloat16 [256, 4096], P('gz', ('gy', 'gx')), may hold values from -14 to 14, as said below
- tiles: bfloat16 [32, 32, 128, 128], P('gx', 'gy'), may hold values from -0.5 to 0.5
- block_mask: int32 [32, 32], P('gx', 'gy'), may hold values from 0 to 1, as said below
- tile_counts: int32 [32], P('gx'), may hold values from 1 to 32, as said below
- weight: bfloat16 [256, 256], replicated, may hold values from -0.375 to 0.375
- gamma: float32 [256], P('gz'), may hold values from 0.5 to 2
- beta: float32 [256], P('gz'), may hold values from -3 to 3
Outputs:
- normed: bfloat16 [256, 4096], P('gz', ('gx', 'gy'))
Inputs may be any that keep to these rules, and one draw needn't show every extreme that they name: `features`: channels along dimension 0, nodes along dimension 1. `block_mask`: 1 where block row and block column meet in a nonzero block, else 0; the diagonal is 1. tile_counts[r] is the number of ones in row r of block_mask.
All inputs are finite; a program needn't handle non-finite values.
Results may differ from a plain program's by a relative error of at most 0.013.
Values may be sent and summed in bfloat16 or wider, within the bound.
A program may use at most 64 MiB of HBM per device.

v0:
```python
import jax
import jax.numpy as jnp
from jax import lax
from jax.sharding import PartitionSpec as P


def body(features, tiles, block_mask, tile_counts, weight, gamma, beta):
    panel = lax.all_gather(features, "gx", axis=1, tiled=True)
    local_ch = panel.shape[0]
    rows_blk = tiles.shape[0]
    cols_blk = tiles.shape[1]
    tile_len = tiles.shape[2]
    panels = panel.reshape(local_ch, cols_blk, tile_len)
    prods = jnp.einsum("fcn,rcmn->frcm", panels, tiles, preferred_element_type=jnp.float32)
    share = block_mask.astype(jnp.float32) / tile_counts.astype(jnp.float32)[:, None]
    partial_value = jnp.einsum("frcm,rc->frm", prods, share).reshape(local_ch, rows_blk * tile_len)
    summed = lax.psum(partial_value, "gy")
    width = rows_blk * tile_len // lax.axis_size("gy")
    agg = lax.dynamic_slice_in_dim(summed, lax.axis_index("gy") * width, width, 1)
    agg = agg.astype(jnp.bfloat16)
    offset = lax.axis_index("gz") * local_ch
    full = lax.all_gather(agg, "gz", axis=0, tiled=True)
    w_cols = lax.dynamic_slice_in_dim(weight, offset, local_ch, 1)
    z_vals = jnp.einsum("co,cn->on", w_cols, full, preferred_element_type=jnp.float32)
    total = z_vals.shape[1] * lax.axis_size(("gx", "gy"))
    sums, squares = lax.psum(
        (jnp.sum(z_vals, axis=1), jnp.sum(z_vals * z_vals, axis=1)), ("gx", "gy")
    )
    mean = sums / total
    var = squares / total - mean * mean
    centered = z_vals - mean[:, None]
    scaled = gamma[:, None] * centered * lax.rsqrt(var + 1e-05)[:, None] + beta[:, None]
    return jnp.maximum(scaled, 0.0).astype(jnp.bfloat16)


def solution(mesh):
    in_specs = (
        P("gz", ("gy", "gx")),
        P("gx", "gy", None, None),
        P("gx", "gy"),
        P("gx"),
        P(),
        P("gz"),
        P("gz"),
    )
    out_specs = P("gz", ("gx", "gy"))
    return jax.shard_map(body, mesh=mesh, in_specs=in_specs, out_specs=out_specs, check_vma=False)
```

profile of v0, /device:TPU:0, one launch (start us, length us, event | category | flops | bytes accessed | tf_op | source)
XLA Modules:
  0.0 57.3 jit_solution(9171550169248883873)
XLA Ops:
  0.0 0.0 copy-start
  0.0 0.7 %convert_element_type.13 = f32[16]{0:T(128)S(1)} convert(s32[16]{0:T(128)} %param.10) | non-fusion elementwise | flops 16 | bytes 128 | tf_op jit(solution)/shard_map/convert_element_type | solution.py:15
  0.7 0.7 %divide_bitcast_fusion = bf16[16,8,1,1]{0,1,2,3:T(8,128)(2,1)S(1)} fusion(s32[16,8]{0,1:T(8,128)} %param.9, f32[16]{0:T(128)S(1)} %convert_element_type.13), kind=kLoop, calls=%fused_computation.12 | loop fusion | flops 384 | bytes 832 | tf_op jit(solution)/shard_map/div | solution.py:15
  1.4 0.1 copy.12
  1.5 6.1 %all_gather.6 = bf16[64,1024]{1,0:T(8,128)(2,1)S(1)} all-gather(bf16[64,512]{1,0:T(8,128)(2,1)} %param.7), channel_id=1, replica_groups=mesh['gx'=2,'gy'=4,'gz'=4] {'gx'}, dimensions={1}, use_global_device_ids=true | all-gather | bytes 196608 | tf_op jit(solution)/shard_map/all_gather | solution.py:8
  7.6 3.8 %fusion.4 = bf16[64,16,8,128]{3,0,1,2:T(8,128)(2,1)S(1)} fusion(bf16[16,8,128,128]{3,2,1,0:T(8,128)(2,1)} %param.8, bf16[64,8,128,1]{2,1,0,3:T(8,128)(2,1)S(1)} %bitcast.19), kind=kOutput, calls=%fused_computation.4 | convolution fusion | flops 268435456 | bytes 6422528 | tf_op jit(solution)/shard_map/fcn,rcmn->frcm/dot_general | solution.py:14
  11.4 1.4 %fusion = f32[16,1,64,128]{3,1,2,0:T(1,128)S(1)} fusion(bf16[16,8,1,1]{1,2,3,0:T(2,128)(2,1)S(1)} %copy.12, bf16[64,16,8,128]{3,0,1,2:T(8,128)(2,1)S(1)} %fusion.4), kind=kOutput, calls=%fused_computation | convolution fusion | flops 2097152 | bytes 2621696 | tf_op jit(solution)/shard_map/frcm,rc->frm/dot_general | solution.py:16
  12.8 0.0 copy-start.1
  12.8 0.0 copy-start.2
  12.8 0.3 copy.14
  13.2 0.2 copy.28
  13.3 16.7 %all-reduce.2 = bf16[64,2048]{1,0:T(8,128)(2,1)S(1)} all-reduce(f32[64,2048]{1,0:T(8,128)S(1)} %bitcast.18), channel_id=1, replica_groups=mesh['gx'=2,'gy'=4,'gz'=4] {'gy'}, use_global_device_ids=true, to_apply=%region_0.0 | all-reduce | flops 131072 | bytes 786432 | tf_op jit(solution)/shard_map/psum | solution.py:17
  30.1 14.2 %all_gather.7 = bf16[256,512]{1,0:T(8,128)(2,1)S(1)} all-gather(bf16[64,512]{1,0:T(8,128)(2,1)S(1)} %dynamic-slice_convert_fusion), channel_id=1, replica_groups=mesh['gx'=2,'gy'=4,'gz'=4] {'gz'}, dimensions={0}, use_global_device_ids=true | all-gather | bytes 327680 | tf_op jit(solution)/shard_map/all_gather | solution.py:22
  44.3 0.0 copy-done
  44.3 0.4 fusion.11
  44.7 11.8 %all-reduce = (f32[64]{0:T(128)S(1)}, f32[64]{0:T(128)S(1)}) all-reduce(f32[64]{0:T(128)S(1)} %get-tuple-element.6, f32[64]{0:T(128)S(1)} %get-tuple-element.5), channel_id=1, replica_groups=mesh['gx'=2,'gy'=4,'gz'=4] {'gx','gy'}, use_global_device_ids=true, to_apply=%region_4.0 | all-reduce | flops 128 | bytes 1024 | tf_op jit(solution)/shard_map/psum | solution.py:26
  56.5 0.0 copy-done.1
  56.5 0.0 copy-done.2
  56.5 0.7 %maximum_convert_fusion = bf16[64,512]{1,0:T(8,128)(2,1)} fusion(f32[64,512]{1,0:T(8,128)S(1)} %get-tuple-element.11, f32[64]{0:T(128)S(1)} %copy-done.1, f32[64]{0:T(128)S(1)} %get-tuple-element.10, f32[64]{0:T(128)S(1)} %get-tuple-element.9, f32[64]{0:T(128)S(1)} %copy-done.2), kind=kLoop, calls=%fused_computation.7 | loop fusion | flops 196608 | bytes 197632 | tf_op jit(solution)/shard_map/convert_element_type | solution.py:33
  (3 shorter events, 0.0 us)
Async XLA Ops:
  0.0 44.3 %copy-start = (bf16[256,256]{1,0:T(8,128)(2,1)S(1)}, bf16[256,256]{1,0:T(8,128)(2,1)}, u32[]{:S(2)}) copy-start(bf16[256,256]{1,0:T(8,128)(2,1)} %param.11) | copy-start | bytes 393220
  12.8 43.7 %copy-start.1 = (f32[64]{0:T(128)S(1)}, f32[64]{0:T(128)}, u32[]{:S(2)}) copy-start(f32[64]{0:T(128)} %param.13) | copy-start | bytes 772
  12.8 43.7 %copy-start.2 = (f32[64]{0:T(128)S(1)}, f32[64]{0:T(128)}, u32[]{:S(2)}) copy-start(f32[64]{0:T(128)} %param.12) | copy-start | bytes 772
where the time goes:
time: 57.5 us; the launch traced here: 57.3 us
  blocking collectives  48.9 us (85%)
  matrix products  5.54 us (10%)
  other arithmetic  2.13 us (4%)
  local copies, waits for them, and re-layouts  0.61 us (1%)
    psum x1, blocking collectives, body(): summed = lax.psum(partial_value, 'gy')  16.7 us
    all_gather x1, blocking collectives, body(): full = lax.all_gather(agg, 'gz', axis=0, tiled=True)  14.2 us
    psum x1, blocking collectives, body(): lax.psum((jnp.sum(z_vals, axis=1), jnp.sum(z_vals * z_vals, axis=1)), ('g...  11.8 us
    all_gather x1, blocking collectives, body(): panel = lax.all_gather(features, 'gx', axis=1, tiled=True)  6.13 us
    dot_general x1, matrix products, body(): jnp.einsum('fcn,rcmn->frcm', panels, tiles, preferred_element_type=jnp.fl...  3.75 us
    dot_general x1, matrix products, body(): jnp.einsum('frcm,rc->frm', prods, share)  1.42 us

commit v1 on v0

--- a/solution.py
+++ b/solution.py
@@ -19,7 +19,12 @@
     agg = lax.dynamic_slice_in_dim(summed, lax.axis_index("gy") * width, width, 1)
     agg = agg.astype(jnp.bfloat16)
     offset = lax.axis_index("gz") * local_ch
-    full = lax.all_gather(agg, "gz", axis=0, tiled=True)
+    ring = [agg]
+    for hop in range(3):
+        ring.append(lax.ppermute(ring[-1], "gz", [(dev, (dev + 1) % 4) for dev in range(4)]))
+    full = jnp.roll(
+        jnp.concatenate(ring[::-1], axis=0), (lax.axis_index("gz") + 1) * ring[0].shape[0], axis=0
+    )
     w_cols = lax.dynamic_slice_in_dim(weight, offset, local_ch, 1)
     z_vals = jnp.einsum("co,cn->on", w_cols, full, preferred_element_type=jnp.float32)
     total = z_vals.shape[1] * lax.axis_size(("gx", "gy"))

time: 57.5 us -> 61.6 us (1.071)
  waiting for transfers between devices: 0 us -> 16.5 us
  blocking collectives: 48.9 us -> 34.7 us
  starting transfers between devices: 0 us -> 1.74 us
    ppermute x0 -> x3, waiting for transfers between devices: none -> 16.5 us  [body(): lax.ppermute(ring[-1], 'gz', [(dev, (dev + 1) % 4) for dev in range(4)])]
    all_gather x1 -> x0, blocking collectives: 14.2 us -> none  [body(): full = lax.all_gather(agg, 'gz', axis=0, tiled=True)]
    ppermute x0 -> x3, starting transfers between devices: none -> 1.74 us  [body(): lax.ppermute(ring[-1], 'gz', [(dev, (dev + 1) % 4) for dev in range(4)])]
  transfers between devices with their start and end apart: 0 -> 3, of which waited for: 0 -> 3; matrix products, arithmetic and copies ran while one was open for 0% -> 0% of each run, Pallas kernels for 0% -> 0%
where the time goes in v1:
time: 61.6 us; the launch traced here: 61.4 us
  blocking collectives  34.7 us (56%)
  waiting for transfers between devices  16.5 us (27%)
  matrix products  5.54 us (9%)
  other arithmetic  2.13 us (3%)
  starting transfers between devices  1.74 us (3%)
  local copies, waits for them, and re-layouts  0.68 us (1%)
    psum x1, blocking collectives, body(): summed = lax.psum(partial_value, 'gy')  16.7 us
    ppermute x3, waiting for transfers between devices, body(): lax.ppermute(ring[-1], 'gz', [(dev, (dev + 1) % 4) for dev in range(4)])  16.5 us
    psum x1, blocking collectives, body(): lax.psum((jnp.sum(z_vals, axis=1), jnp.sum(z_vals * z_vals, axis=1)), ('g...  11.8 us
    all_gather x1, blocking collectives, body(): panel = lax.all_gather(features, 'gx', axis=1, tiled=True)  6.13 us
    dot_general x1, matrix products, body(): jnp.einsum('fcn,rcmn->frcm', panels, tiles, preferred_element_type=jnp.fl...  3.75 us
    ppermute x3, starting transfers between devices, body(): lax.ppermute(ring[-1], 'gz', [(dev, (dev + 1) % 4) for dev in range(4)])  1.74 us
    dot_general x1, matrix products, body(): jnp.einsum('frcm,rc->frm', prods, share)  1.42 us
  transfers between devices with their start and end apart: 3, of which 3 were waited for; matrix products, arithmetic and copies ran while one was open for 0% of the time, Pallas kernels for 0%

profile of v1, /device:TPU:0, one launch (start us, length us, event | category | flops | bytes accessed | tf_op | source)
XLA Modules:
  0.0 61.4 jit_solution(4794866651375266219)
XLA Ops:
  0.0 0.0 copy-start
  0.0 0.7 %convert_element_type.13 = f32[16]{0:T(128)S(1)} convert(s32[16]{0:T(128)} %param.10) | non-fusion elementwise | flops 16 | bytes 128 | tf_op jit(solution)/shard_map/convert_element_type | solution.py:15
  0.7 0.7 %divide_bitcast_fusion = bf16[16,8,1,1]{0,1,2,3:T(8,128)(2,1)S(1)} fusion(s32[16,8]{0,1:T(8,128)} %param.9, f32[16]{0:T(128)S(1)} %convert_element_type.13), kind=kLoop, calls=%fused_computation.21 | loop fusion | flops 384 | bytes 832 | tf_op jit(solution)/shard_map/div | solution.py:15
  1.4 0.1 copy.12
  1.5 6.1 %all_gather.3 = bf16[64,1024]{1,0:T(8,128)(2,1)S(1)} all-gather(bf16[64,512]{1,0:T(8,128)(2,1)} %param.7), channel_id=1, replica_groups=mesh['gx'=2,'gy'=4,'gz'=4] {'gx'}, dimensions={1}, use_global_device_ids=true | all-gather | bytes 196608 | tf_op jit(solution)/shard_map/all_gather | solution.py:8
  7.6 3.8 %fusion.4 = bf16[64,16,8,128]{3,0,1,2:T(8,128)(2,1)S(1)} fusion(bf16[16,8,128,128]{3,2,1,0:T(8,128)(2,1)} %param.8, bf16[64,8,128,1]{2,1,0,3:T(8,128)(2,1)S(1)} %bitcast.18), kind=kOutput, calls=%fused_computation.4 | convolution fusion | flops 268435456 | bytes 6422528 | tf_op jit(solution)/shard_map/fcn,rcmn->frcm/dot_general | solution.py:14
  11.4 1.4 %fusion = f32[16,1,64,128]{3,1,2,0:T(1,128)S(1)} fusion(bf16[16,8,1,1]{1,2,3,0:T(2,128)(2,1)S(1)} %copy.12, bf16[64,16,8,128]{3,0,1,2:T(8,128)(2,1)S(1)} %fusion.4), kind=kOutput, calls=%fused_computation | convolution fusion | flops 2097152 | bytes 2621696 | tf_op jit(solution)/shard_map/frcm,rc->frm/dot_general | solution.py:16
  12.8 0.0 copy-start.1
  12.8 0.0 copy-start.2
  12.8 0.3 copy.14
  13.2 0.2 copy.28
  13.3 16.7 %all-reduce.2 = bf16[64,2048]{1,0:T(8,128)(2,1)S(1)} all-reduce(f32[64,2048]{1,0:T(8,128)S(1)} %bitcast.17), channel_id=1, replica_groups=mesh['gx'=2,'gy'=4,'gz'=4] {'gy'}, use_global_device_ids=true, to_apply=%region_0.0 | all-reduce | flops 131072 | bytes 786432 | tf_op jit(solution)/shard_map/psum | solution.py:17
  30.1 1.7 %collective-permute-start = (bf16[64,512]{1,0:T(8,128)(2,1)S(1)}, bf16[64,512]{1,0:T(8,128)(2,1)S(1)}, u32[]{:S(2)}, u32[]{:S(2)}) collective-permute-start(bf16[64,512]{1,0:T(8,128)(2,1)S(1)} %dynamic-slice_convert_fusion), channel_id=1, source_target_pairs={{0,1},{1,2},{2,3},{3,0},{4,5},{5,6},{6,7},{7,4},{8,9},{9,10},{10,1... | collective-permute-start | bytes 196616 | tf_op jit(solution)/shard_map/ppermute | solution.py:24
  31.8 4.4 %collective-permute-done = bf16[64,512]{1,0:T(8,128)(2,1)S(1)} collective-permute-done((bf16[64,512]{1,0:T(8,128)(2,1)S(1)}, bf16[64,512]{1,0:T(8,128)(2,1)S(1)}, u32[]{:S(2)}, u32[]{:S(2)}) %collective-permute-start) | collective-permute-done | bytes 65568 | tf_op jit(solution)/shard_map/ppermute | solution.py:24
  36.2 0.0 collective-permute-start.1
  36.2 6.1 %collective-permute-done.1 = bf16[64,512]{1,0:T(8,128)(2,1)S(1)} collective-permute-done((bf16[64,512]{1,0:T(8,128)(2,1)S(1)}, bf16[64,512]{1,0:T(8,128)(2,1)S(1)}, u32[]{:S(2)}, u32[]{:S(2)}) %collective-permute-start.1) | collective-permute-done | bytes 65568 | tf_op jit(solution)/shard_map/ppermute | solution.py:24
  42.3 0.0 collective-permute-start.2
  42.3 6.1 %collective-permute-done.2 = bf16[64,512]{1,0:T(8,128)(2,1)S(1)} collective-permute-done((bf16[64,512]{1,0:T(8,128)(2,1)S(1)}, bf16[64,512]{1,0:T(8,128)(2,1)S(1)}, u32[]{:S(2)}, u32[]{:S(2)}) %collective-permute-start.2) | collective-permute-done | bytes 65568 | tf_op jit(solution)/shard_map/ppermute | solution.py:24
  48.5 0.0 copy-done
  48.5 0.4 fusion.12
  48.9 11.8 %all-reduce = (f32[64]{0:T(128)S(1)}, f32[64]{0:T(128)S(1)}) all-reduce(f32[64]{0:T(128)S(1)} %get-tuple-element.6, f32[64]{0:T(128)S(1)} %get-tuple-element.5), channel_id=1, replica_groups=mesh['gx'=2,'gy'=4,'gz'=4] {'gx','gy'}, use_global_device_ids=true, to_apply=%region_4.5 | all-reduce | flops 128 | bytes 1024 | tf_op jit(solution)/shard_map/psum | solution.py:31
  60.7 0.0 copy-done.1
  60.7 0.0 copy-done.2
  60.7 0.7 %maximum_convert_fusion = bf16[64,512]{1,0:T(8,128)(2,1)} fusion(f32[64,512]{1,0:T(8,128)S(1)} %get-tuple-element.11, f32[64]{0:T(128)S(1)} %copy-done.1, f32[64]{0:T(128)S(1)} %get-tuple-element.10, f32[64]{0:T(128)S(1)} %get-tuple-element.9, f32[64]{0:T(128)S(1)} %copy-done.2), kind=kLoop, calls=%fused_computation.9 | loop fusion | flops 196608 | bytes 197632 | tf_op jit(solution)/shard_map/convert_element_type | solution.py:38
  (11 shorter events, 0.1 us)
Async XLA Ops:
  0.0 48.5 %copy-start = (bf16[256,256]{1,0:T(8,128)(2,1)S(1)}, bf16[256,256]{1,0:T(8,128)(2,1)}, u32[]{:S(2)}) copy-start(bf16[256,256]{1,0:T(8,128)(2,1)} %param.11) | copy-start | bytes 393220
  12.8 47.9 %copy-start.1 = (f32[64]{0:T(128)S(1)}, f32[64]{0:T(128)}, u32[]{:S(2)}) copy-start(f32[64]{0:T(128)} %param.13) | copy-start | bytes 772
  12.8 47.8 %copy-start.2 = (f32[64]{0:T(128)S(1)}, f32[64]{0:T(128)}, u32[]{:S(2)}) copy-start(f32[64]{0:T(128)} %param.12) | copy-start | bytes 772
  30.1 6.1 %collective-permute-start = (bf16[64,512]{1,0:T(8,128)(2,1)S(1)}, bf16[64,512]{1,0:T(8,128)(2,1)S(1)}, u32[]{:S(2)}, u32[]{:S(2)}) collective-permute-start(bf16[64,512]{1,0:T(8,128)(2,1)S(1)} %dynamic-slice_convert_fusion), channel_id=1, source_target_pairs={{0,1},{1,2},{2,3},{3,0},{4,5},{5,6},{6,7},{7,4},{8,9},{9,10},{10,1... | collective-permute-start | bytes 196616 | tf_op jit(solution)/shard_map/ppermute | solution.py:24
  36.2 6.1 %collective-permute-start.1 = (bf16[64,512]{1,0:T(8,128)(2,1)S(1)}, bf16[64,512]{1,0:T(8,128)(2,1)S(1)}, u32[]{:S(2)}, u32[]{:S(2)}) collective-permute-start(bf16[64,512]{1,0:T(8,128)(2,1)S(1)} %collective-permute-done), channel_id=1, source_target_pairs={{0,1},{1,2},{2,3},{3,0},{4,5},{5,6},{6,7},{7,4},{8,9},{9,10},{10,1... | collective-permute-start | bytes 196616 | tf_op jit(solution)/shard_map/ppermute | solution.py:24
  42.3 6.1 %collective-permute-start.2 = (bf16[64,512]{1,0:T(8,128)(2,1)S(1)}, bf16[64,512]{1,0:T(8,128)(2,1)S(1)}, u32[]{:S(2)}, u32[]{:S(2)}) collective-permute-start(bf16[64,512]{1,0:T(8,128)(2,1)S(1)} %collective-permute-done.1), channel_id=1, source_target_pairs={{0,1},{1,2},{2,3},{3,0},{4,5},{5,6},{6,7},{7,4},{8,9},{9,10},{10,1... | collective-permute-start | bytes 196616 | tf_op jit(solution)/shard_map/ppermute | solution.py:24
